TPU v7x, 32 devices: a whole 2x2x4 slice. The times are simulated.
32 devices in a mesh: dp: 8 (over z, x), mp: 4 (over y, core).
Axes of the slice: x: 2, y: 2, z: 4, core: 2. Of those that a mesh axis runs over, the one named last changes fastest.
Arguments:
- hidden: bfloat16 [8, 512, 4608], P('dp', 'mp'), may hold values from -6 to 6
- lengths: int32 [8], P('dp'), may hold values from 64 to 512
- norm_gain: float32 [4608], replicated, may hold values from 0.25 to 1.75
- w_query: bfloat16 [4608, 2048], P('dp', 'mp'), may hold values from -0.09375 to 0.09375
- w_key: bfloat16 [4608, 1024], P('dp', 'mp'), may hold values from -0.09375 to 0.09375
- w_value: bfloat16 [4608, 1024], P('dp', 'mp'), may hold values from -0.09375 to 0.09375
- w_out: bfloat16 [2048, 4608], P('mp', 'dp'), may hold values from -0.125 to 0.125
- post_gain: float32 [4608], replicated, may hold values from 0.25 to 1.75
Outputs:
- mixed: bfloat16 [8, 512, 4608], P('dp', 'mp')
- key_cache: bfloat16 [8, 512, 1024], P('dp', None, 'mp')
- value_cache: bfloat16 [8, 512, 1024], P('dp', None, 'mp')
All inputs are finite; a program needn't handle non-finite values.
Results may differ from a plain program's by a relative error of at most 0.01.
Values may be sent and summed in bfloat16 or wider, within the bound.
A program may use at most 128 MiB of HBM per device.

v0:
```python
import jax
import jax.numpy as jnp
from jax import lax
from jax.sharding import PartitionSpec as P

HD = 128


def rotate(values, positions):
    half = values.shape[-1] // 2
    freqs = 10000.0 ** (-jnp.arange(half, dtype=jnp.float32) / half)
    angles = positions.astype(jnp.float32)[:, None] * freqs[None, :]
    cosine = jnp.cos(angles)[:, None, :]
    sine = jnp.sin(angles)[:, None, :]
    first = values[..., :half]
    second = values[..., half:]
    return jnp.concatenate(
        [first * cosine - second * sine, second * cosine + first * sine], axis=-1
    )


def attend(query_rows, key_rows, value_rows, row_index, length):
    score = jnp.einsum("qkgd,tkd->kgqt", query_rows, key_rows, preferred_element_type=jnp.float32)
    score = 50.0 * jnp.tanh(score / 50.0)
    key_index = jnp.arange(key_rows.shape[0], dtype=jnp.int32)
    keep = (key_index[None, :] <= row_index[:, None]) & (key_index[None, :] < length)
    score = jnp.where(keep[None, None], score, -1e30)
    top = jnp.max(score, axis=-1, keepdims=True)
    expo = jnp.exp(score - top)
    weights = (expo / jnp.sum(expo, axis=-1, keepdims=True)).astype(jnp.bfloat16)
    return jnp.einsum(
        "kgqt,tkd->qkgd", weights, value_rows, preferred_element_type=jnp.float32
    ).astype(jnp.bfloat16)


def local(hidden, lengths, norm_gain, w_query, w_key, w_value, w_out, post_gain):
    rollouts, local_len, width = hidden.shape
    maxlen = local_len * lax.axis_size("mp")
    q_heads = w_query.shape[1] // HD
    kv_heads = w_key.shape[1] // HD
    group = q_heads // kv_heads
    rows_f = hidden.astype(jnp.float32)
    normed = (
        rows_f * lax.rsqrt(jnp.mean(rows_f * rows_f, axis=-1, keepdims=True) + 1e-06) * norm_gain
    ).astype(jnp.bfloat16)
    gathered = lax.all_gather(normed, "mp", axis=1, tiled=True)
    flat = gathered.reshape(rollouts * maxlen, width)
    pieces = (
        lax.all_gather(w_query, "dp", axis=0, tiled=True),
        lax.all_gather(w_key, "dp", axis=0, tiled=True),
        lax.all_gather(w_value, "dp", axis=0, tiled=True),
    )
    qraw, kraw, vraw = tuple(
        (jnp.dot(flat, piece, preferred_element_type=jnp.float32) for piece in pieces)
    )
    positions = jnp.arange(maxlen, dtype=jnp.int32)
    query = (
        rotate(qraw.reshape(rollouts, maxlen, q_heads, HD), positions) * 144.0 ** (-0.5)
    ).astype(jnp.bfloat16)
    key = rotate(kraw.reshape(rollouts, maxlen, kv_heads, HD), positions).astype(jnp.bfloat16)
    value = vraw.reshape(rollouts, maxlen, kv_heads, HD).astype(jnp.bfloat16)
    grouped = query.reshape(rollouts, maxlen, kv_heads, group, HD)
    length = lengths[0]
    outputs = [attend(grouped[0], key[0], value[0], positions, length)]
    attended = jnp.stack(outputs).reshape(rollouts * maxlen, q_heads * HD)
    partial_value = (
        jnp.dot(
            attended,
            lax.all_gather(w_out, "dp", axis=1, tiled=True),
            preferred_element_type=jnp.float32,
        )
        .astype(jnp.bfloat16)
        .astype(jnp.float32)
    )
    projected = lax.psum_scatter(
        partial_value.reshape(rollouts, maxlen, width).astype(jnp.bfloat16),
        "mp",
        scatter_dimension=1,
        tiled=True,
    ).astype(jnp.float32)
    post = (
        projected
        * lax.rsqrt(jnp.mean(projected * projected, axis=-1, keepdims=True) + 1e-06)
        * post_gain
    )
    own_rows = lax.axis_index("mp") * local_len + jnp.arange(local_len, dtype=jnp.int32)
    live_local = (own_rows[None, :] < lengths[:, None])[:, :, None]
    mixed = jnp.where(live_local, rows_f + post, 0.0).astype(jnp.bfloat16)
    live_all = (positions[None, :] < lengths[:, None])[:, :, None]
    key_cache = jnp.where(
        live_all, key.reshape(rollouts, maxlen, kv_heads * HD), jnp.zeros((), jnp.bfloat16)
    )
    value_cache = jnp.where(
        live_all, value.reshape(rollouts, maxlen, kv_heads * HD), jnp.zeros((), jnp.bfloat16)
    )
    return (mixed, key_cache, value_cache)


def solution(mesh):
    return jax.shard_map(
        local,
        mesh=mesh,
        in_specs=(
            P("dp", "mp", None),
            P("dp"),
            P(),
            P("dp", "mp"),
            P("dp", "mp"),
            P("dp", "mp"),
            P("mp", "dp"),
            P(),
        ),
        out_specs=(P("dp", "mp", None), P("dp", None, "mp"), P("dp", None, "mp")),
        check_vma=False,
    )
```

profile of v0, /device:TPU:0, one launch (start us, length us, event | category | flops | bytes accessed | tf_op | source)
XLA Modules:
  0.0 381.2 jit_solution(8354099245536206741)
XLA Ops:
  7.2 0.0 all-gather.10.cloned.1.call-start
  7.2 0.7 all-gather.10.cloned.1.call-update
  7.9 0.0 all-gather.8.cloned.1.call-start
  7.9 0.7 all-gather.8.cloned.1.call-update
  8.6 0.0 all-gather.6.cloned.1.call-start
  8.7 1.6 fusion.11
  10.3 2.6 fusion.13
  12.9 0.0 all-gather.6.cloned.1.call-update
  12.9 0.0 all-gather.12.cloned.1.call-start
  13.0 0.5 all-gather.12.cloned.1.call-update
  13.5 0.0 all-gather.14.cloned.1.call-start
  13.6 0.5 all-gather.14.cloned.1.call-update
  14.1 0.0 reduce-scatter.2.cloned.1.call-start
  14.8 0.8 fusion.32
  15.7 0.5 multiply_cosine_fusion
  16.2 48.5 %all-gather.10.cloned.1.call-done = bf16[4608,256]{1,0:T(8,128)(2,1)} async-done(((bf16[576,256]{1,0:T(8,128)(2,1)}), bf16[4608,256]{1,0:T(8,128)(2,1)}) %all-gather.10.cloned.1.call-update) | async-done | bytes 2359312 | tf_op jit(solution)/shard_map/all_gather | solution.py:50
  64.7 4.3 %copy.12 = bf16[256,4608]{1,0:T(8,128)(2,1)} copy(bf16[256,4608]{0,1:T(8,128)(2,1)} %bitcast.78) | data formatting | bytes 4718592 | tf_op jit(solution)/shard_map/dot_general | solution.py:54
  69.0 48.2 %all-gather.8.cloned.1.call-done = bf16[4608,256]{1,0:T(8,128)(2,1)} async-done(((bf16[576,256]{1,0:T(8,128)(2,1)}), bf16[4608,256]{1,0:T(8,128)(2,1)}) %all-gather.8.cloned.1.call-update) | async-done | bytes 2359312 | tf_op jit(solution)/shard_map/all_gather | solution.py:51
  117.3 2.8 copy.11
  120.1 35.3 %all-gather.6.cloned.1.call-done = bf16[1,512,4608]{2,1,0:T(8,128)(2,1)} async-done(((bf16[1,128,4608]{2,1,0:T(8,128)(2,1)}), bf16[1,512,4608]{2,1,0:T(8,128)(2,1)}) %all-gather.6.cloned.1.call-update) | async-done | bytes 4718608 | tf_op jit(solution)/shard_map/all_gather | solution.py:46
  155.4 0.0 copy-start.3
  155.4 4.6 %fusion.25 = f32[1,512,2,128]{1,3,2,0:T(8,128)S(1)} fusion(bf16[2,128,4608]{2,1,0:T(8,128)(2,1)} %bitcast.81, bf16[1,512,4608]{2,1,0:T(8,128)(2,1)} %all-gather.6.cloned.1.call-done), kind=kOutput, calls=%fused_computation.32 | convolution fusion | flops 1207959552 | bytes 7602176 | tf_op jit(solution)/shard_map/dot_general | solution.py:54
  160.1 0.1 subtract_convert_fusion
  160.2 0.0 copy-done.3
  160.2 1.4 fusion.28
  161.6 75.2 %all-gather.12.cloned.1.call-done = bf16[4608,512]{1,0:T(8,128)(2,1)} async-done(((bf16[576,512]{1,0:T(8,128)(2,1)}), bf16[4608,512]{1,0:T(8,128)(2,1)}) %all-gather.12.cloned.1.call-update) | async-done | bytes 4718608 | tf_op jit(solution)/shard_map/all_gather | solution.py:49
  236.8 6.7 %copy.13 = bf16[512,4608]{1,0:T(8,128)(2,1)} copy(bf16[512,4608]{0,1:T(8,128)(2,1)} %bitcast.76) | data formatting | bytes 9437184 | tf_op jit(solution)/shard_map/dot_general | solution.py:54
  243.5 6.4 %fusion.21 = f32[1,512,4,128]{1,3,2,0:T(8,128)S(1)} fusion(bf16[4,128,4608]{2,1,0:T(8,128)(2,1)} %bitcast.77, bf16[1,512,4608]{2,1,0:T(8,128)(2,1)} %all-gather.6.cloned.1.call-done), kind=kOutput, calls=%fused_computation.30 | convolution fusion | flops 2415919104 | bytes 10485760 | tf_op jit(solution)/shard_map/dot_general | solution.py:54
  249.9 0.2 multiply_subtract_fusion
  250.1 0.0 copy-start.1
  250.1 0.3 copy.15
  250.4 0.3 copy.14
  250.8 0.3 fusion.31
  251.1 0.0 copy-done.1
  251.2 1.9 fusion.53
  253.1 2.4 fusion.24
  255.5 61.1 %all-gather.14.cloned.1.call-done = bf16[512,4608]{0,1:T(8,128)(2,1)} async-done(((bf16[512,576]{0,1:T(8,128)(2,1)}), bf16[512,4608]{0,1:T(8,128)(2,1)}) %all-gather.14.cloned.1.call-update) | async-done | bytes 4718608 | tf_op jit(solution)/shard_map/all_gather | solution.py:69
  316.6 6.7 %fusion.1 = bf16[1,512,4608]{2,1,0:T(8,128)(2,1)} fusion(bf16[512,512]{0,1:T(8,128)(2,1)S(1)} %bitcast.90, bf16[512,4608]{0,1:T(8,128)(2,1)} %all-gather.14.cloned.1.call-done), kind=kOutput, calls=%fused_computation.2 | convolution fusion | flops 2418278400 | bytes 9961472 | tf_op jit(solution)/shard_map/dot_general | solution.py:67
  323.3 0.0 copy-start
  323.3 0.0 copy-start.2
  323.3 0.0 reduce-scatter.2.cloned.1.call-update
  323.4 0.1 copy.19
  323.5 0.1 copy.18
  323.7 0.9 broadcast_select_fusion
  324.6 45.2 %reduce-scatter.2.cloned.1.call-done = bf16[1,128,4608]{2,1,0:T(8,128)(2,1)} async-done(((bf16[1,512,4608]{2,1,0:T(8,128)(2,1)}), bf16[1,128,4608]{2,1,0:T(8,128)(2,1)}) %reduce-scatter.2.cloned.1.call-update) | async-done | bytes 1179664 | tf_op jit(solution)/shard_map/reduce_scatter | solution.py:75
  369.8 1.6 fusion.9
  371.4 0.0 copy-done
  371.4 0.0 copy-done.2
  371.4 2.9 fusion.15
  (7 shorter events, 0.1 us)
Async XLA Ops:
  7.2 57.6 %all-gather.10.cloned.1.call-start = ((), (), s32[]{:S(2)}) async-start(), calls=%async_computation.3 | async-start | bytes 2654208 | tf_op jit(solution)/shard_map/all_gather | solution.py:50
  7.9 109.4 %all-gather.8.cloned.1.call-start = ((), (), s32[]{:S(2)}) async-start(), calls=%async_computation.2 | async-start | bytes 2654208 | tf_op jit(solution)/shard_map/all_gather | solution.py:51
  8.6 146.8 %all-gather.6.cloned.1.call-start = ((), (), s32[]{:S(2)}) async-start(), calls=%async_computation.1 | async-start | bytes 5898240 | tf_op jit(solution)/shard_map/all_gather | solution.py:46
  12.9 223.9 %all-gather.12.cloned.1.call-start = ((), (), s32[]{:S(2)}) async-start(), calls=%async_computation.4 | async-start | bytes 5308416 | tf_op jit(solution)/shard_map/all_gather | solution.py:49
  13.5 303.1 %all-gather.14.cloned.1.call-start = ((), (), s32[]{:S(2)}) async-start(), calls=%async_computation.5 | async-start | bytes 5308416 | tf_op jit(solution)/shard_map/all_gather | solution.py:69
  14.1 355.7 %reduce-scatter.2.cloned.1.call-start = ((), (), s32[]{:S(2)}) async-start(), calls=%async_computation.6 | async-start | bytes 5898240 | tf_op jit(solution)/shard_map/reduce_scatter | solution.py:75
  155.4 4.7 %copy-start.3 = (bf16[1,512,4608]{2,1,0:T(8,128)(2,1)S(1)}, bf16[1,512,4608]{2,1,0:T(8,128)(2,1)}, u32[]{:S(2)}) copy-start(bf16[1,512,4608]{2,1,0:T(8,128)(2,1)} %all-gather.6.cloned.1.call-done) | copy-start | bytes 14155780
  250.1 1.0 copy-start.1
  323.3 48.1 %copy-start = (bf16[1,128,4608]{2,1,0:T(8,128)(2,1)S(1)}, bf16[1,128,4608]{2,1,0:T(8,128)(2,1)}, u32[]{:S(2)}) copy-start(bf16[1,128,4608]{2,1,0:T(8,128)(2,1)} %param.8) | copy-start | bytes 3538948
  323.3 48.1 %copy-start.2 = (f32[4608]{0:T(1024)S(1)}, f32[4608]{0:T(1024)}, u32[]{:S(2)}) copy-start(f32[4608]{0:T(1024)} %param.15) | copy-start | bytes 55300
Sparse Core Ops, SparseCore 0:
  10.2 54.5 all-gather.9
  66.9 50.3 all-gather.7
  119.4 35.9 all-gather.5
  157.5 79.3 all-gather.11
  238.9 77.6 all-gather.13
  323.5 46.3 reduce-scatter.1
where the time goes:
time: 382 us; the launch traced here: 381 us
  waiting for transfers between devices  316 us (83%)
  matrix products  23.5 us (6%)
  between operations  14.9 us (4%)
  local copies, waits for them, and re-layouts  14.8 us (4%)
  other arithmetic  11.6 us (3%)
    all_gather x1, waiting for transfers between devices, local(): lax.all_gather(w_query, 'dp', axis=0, tiled=True)  75.2 us
    all_gather x1, waiting for transfers between devices, local(): lax.all_gather(w_out, 'dp', axis=1, tiled=True)  61.1 us
    all_gather x1, waiting for transfers between devices, local(): lax.all_gather(w_key, 'dp', axis=0, tiled=True)  48.5 us
    all_gather x1, waiting for transfers between devices, local(): lax.all_gather(w_value, 'dp', axis=0, tiled=True)  48.2 us
    reduce_scatter x1, waiting for transfers between devices, local(): lax.psum_scatter(partial_value.reshape(rollouts, maxlen, width).astype(jn...  45.2 us
    all_gather x1, waiting for transfers between devices, local(): gathered = lax.all_gather(normed, 'mp', axis=1, tiled=True)  35.3 us
    dot_general x3, local copies, waits for them, and re-layouts, local(): jnp.dot(flat, piece, preferred_element_type=jnp.float32)  13.9 us
    dot_general x3, matrix products, local(): jnp.dot(flat, piece, preferred_element_type=jnp.float32)  12.4 us
  transfers between devices with their start and end apart: 6, of which 6 were waited for; matrix products, arithmetic and copies ran while one was open for 10% of the time, Pallas kernels for 0%

commit v1 on v0

v1 whole, which is shorter than its diff:
```python
import functools

import jax
import jax.numpy as jnp
import numpy as np
from jax import lax
from jax.experimental import pallas as pl
from jax.experimental.pallas import tpu as pltpu
from jax.sharding import PartitionSpec as P

HD = 128
MESH = pl.DeviceIdType.MESH
UP, DOWN, ACROSS = 0, 1, 2


def tables(maxlen):
    half = HD // 2
    freqs = 10000.0 ** (-np.arange(half, dtype=np.float64) / half)
    angles = np.arange(maxlen, dtype=np.float64)[:, None] * freqs[None, :]
    cosine, sine = np.cos(angles), np.sin(angles)
    return (
        np.concatenate([cosine, cosine], axis=1).astype(np.float32),
        np.concatenate([-sine, sine], axis=1).astype(np.float32),
    )


def cut(rows):
    if rows % 32:
        return [None, (0, rows)]
    first = rows // 6 // 16 * 16
    rest = rows - first
    chunk = rest // 2 // 16 * 16
    return [(0, first), (first, chunk), (first + chunk, rest - chunk)]


def kernel(
    n_dp, n_mp, cuts,
    len_ref, hid, ngain, wq, wk, wv, wo, pgain, cos_ref, sin_ref,
    mixed, key_out, val_out,
    wbuf, obuf, nbuf, acc, att, psend, precv,
    load_sem, send_sem, recv_sem, nsend_sem, nrecv_sem, psend_sem, precv_sem,
):
    nz = n_dp // 2
    me, mp = lax.axis_index("dp"), lax.axis_index("mp")
    z, x = me // 2, me % 2
    local_len, width = hid.shape
    maxlen = local_len * n_mp
    fcols = width // n_dp
    qw, kw = wq.shape[1], wk.shape[1]
    q_heads, kv_heads = qw // HD, kw // HD
    can_up, can_down = z < nz - 1, z > 0
    bufs = (wbuf, obuf)

    loads = [
        pltpu.make_async_copy(wq, wbuf.at[me, :, pl.ds(0, qw)], load_sem.at[0]),
        pltpu.make_async_copy(wk, wbuf.at[me, :, pl.ds(qw, kw)], load_sem.at[1]),
        pltpu.make_async_copy(wv, wbuf.at[me, :, pl.ds(qw + kw, kw)], load_sem.at[2]),
        pltpu.make_async_copy(wo, obuf.at[me], load_sem.at[3]),
    ]
    for load in loads:
        load.start()

    barrier = pltpu.get_barrier_semaphore()

    def greet(dp_index, mp_index):
        pl.semaphore_signal(barrier, inc=1, device_id=(dp_index, mp_index), device_id_type=MESH)

    greet(me + 1 - 2 * x, mp)
    for step in range(1, n_mp):
        greet(me, lax.rem(mp + step, n_mp))

    @pl.when(can_up)
    def _():
        greet(me + 2, mp)

    @pl.when(can_down)
    def _():
        greet(me - 2, mp)

    pl.semaphore_wait(
        barrier, n_mp + jnp.where(can_up, 1, 0) + jnp.where(can_down, 1, 0)
    )

    def copy(kind, part, origin, way):
        start, size = cuts[kind][part]
        ref = bufs[kind].at[origin, pl.ds(start, size)]
        target = (me + 2, me - 2, me + 1 - 2 * x)[way]
        return pltpu.make_async_remote_copy(
            src_ref=ref,
            dst_ref=ref,
            send_sem=send_sem.at[kind, part, way, origin],
            recv_sem=recv_sem.at[kind, part, origin],
            device_id=(target, mp),
            device_id_type=MESH,
        )

    def send_chain(kind, part, origin):
        @pl.when(can_up)
        def _():
            copy(kind, part, origin, UP).start()

        @pl.when(can_down)
        def _():
            copy(kind, part, origin, DOWN).start()

    def rest_of(kind):
        return range(1, len(cuts[kind]))

    def send_own(kind):
        if cuts[kind][0]:
            copy(kind, 0, me, ACROSS).start()
        for part in rest_of(kind):
            send_chain(kind, part, me)
            copy(kind, part, me, ACROSS).start()
        if cuts[kind][0]:
            send_chain(kind, 0, me)

    def send_partner(kind):
        if cuts[kind][0]:
            partner = me + 1 - 2 * x
            copy(kind, 0, partner, ACROSS).wait_recv()
            send_chain(kind, 0, partner)

    def relay(kind, k):
        below, above = z - k, z + k
        for part in rest_of(kind):
            @pl.when(below >= 0)
            def _():
                origin = below * 2 + x
                copy(kind, part, origin, UP).wait_recv()

                @pl.when(can_up)
                def _():
                    copy(kind, part, origin, UP).start()

                copy(kind, part, origin, ACROSS).start()

            @pl.when(above < nz)
            def _():
                origin = above * 2 + x
                copy(kind, part, origin, DOWN).wait_recv()

                @pl.when(can_down)
                def _():
                    copy(kind, part, origin, DOWN).start()

                copy(kind, part, origin, ACROSS).start()

        if cuts[kind][0]:
            for column in range(2):
                @pl.when(below >= 0)
                def _():
                    origin = below * 2 + column
                    copy(kind, 0, origin, UP).wait_recv()

                    @pl.when(can_up)
                    def _():
                        copy(kind, 0, origin, UP).start()

                @pl.when(above < nz)
                def _():
                    origin = above * 2 + column
                    copy(kind, 0, origin, DOWN).wait_recv()

                    @pl.when(can_down)
                    def _():
                        copy(kind, 0, origin, DOWN).start()

    def wait_across(kind, origin):
        for part in rest_of(kind):
            copy(kind, part, origin, ACROSS).wait_recv()

    def drain(kind):
        def body(origin, carry):
            oz, ox = origin // 2, origin % 2
            for part in range(len(cuts[kind])):
                if not cuts[kind][part]:
                    continue
                mine = (ox == x) | (part == 0)

                @pl.when(mine & (oz <= z) & can_up)
                def _():
                    copy(kind, part, origin, UP).wait_send()

                @pl.when(mine & (oz >= z) & can_down)
                def _():
                    copy(kind, part, origin, DOWN).wait_send()

                @pl.when((origin == me) if part == 0 else (ox == x))
                def _():
                    copy(kind, part, origin, ACROSS).wait_send()

            return carry

        lax.fori_loop(0, n_dp, body, 0)

    for load in loads[:3]:
        load.wait()
    send_own(0)

    total = jnp.zeros((local_len, 1), jnp.float32)
    for block in range(n_dp):
        rows = hid[:, block * fcols : (block + 1) * fcols].astype(jnp.float32)
        total = total + jnp.sum(rows * rows, axis=-1, keepdims=True)
    scale = lax.rsqrt(total / width + 1e-06)
    for block in range(n_dp):
        span = slice(block * fcols, (block + 1) * fcols)
        rows = hid[:, span].astype(jnp.float32)
        nbuf[mp, block] = (rows * scale * ngain[:, span]).astype(jnp.bfloat16)

    def share(step):
        return pltpu.make_async_remote_copy(
            src_ref=nbuf.at[mp],
            dst_ref=nbuf.at[mp],
            send_sem=nsend_sem.at[step],
            recv_sem=nrecv_sem.at[mp],
            device_id=(me, lax.rem(mp + step, n_mp)),
            device_id_type=MESH,
        )

    def shared(source):
        return pltpu.make_async_remote_copy(
            src_ref=nbuf.at[source],
            dst_ref=nbuf.at[source],
            send_sem=nsend_sem.at[0],
            recv_sem=nrecv_sem.at[source],
            device_id=(me, source),
            device_id_type=MESH,
        )

    for step in range(1, n_mp):
        share(step).start()
    send_partner(0)
    acc[...] = jnp.zeros_like(acc)

    def step_qkv(k, carry):
        relay(0, k)
        return carry

    lax.fori_loop(1, nz, step_qkv, 0)
    loads[3].wait()
    send_own(1)
    for step in range(1, n_mp):
        shared(lax.rem(mp + step, n_mp)).wait_recv()

    def project(i, carry):
        other, k, side = i // (2 * nz), i // 2 % nz, i % 2
        oz = z + k * (2 * side - 1)
        origin = oz * 2 + lax.rem(x + other, 2)

        @pl.when((oz >= 0) & (oz < nz) & ((side == 0) | (k > 0)))
        def _():
            @pl.when(other == 1)
            def _():
                wait_across(0, origin)

            for m in range(n_mp):
                span = slice(m * local_len, (m + 1) * local_len)
                acc[span, :] += jnp.dot(
                    nbuf[m, origin], wbuf[origin], preferred_element_type=jnp.float32
                )

        return carry

    lax.fori_loop(0, 4 * nz, project, 0)
    send_partner(1)

    length = len_ref[0]
    live = lax.broadcasted_iota(jnp.int32, (maxlen, HD), 0) < length

    def rotated(block, span):
        return block * cos_ref[span, :] + pltpu.roll(block, HD // 2, 1) * sin_ref[span, :]

    everything = slice(0, maxlen)
    for h in range(kv_heads):
        cols = slice(h * HD, (h + 1) * HD)
        keys = rotated(acc[:, qw + h * HD : qw + (h + 1) * HD], everything)
        key_out[:, cols] = jnp.where(live, keys, 0.0).astype(jnp.bfloat16)
        values = acc[:, qw + kw + h * HD : qw + kw + (h + 1) * HD]
        val_out[:, cols] = jnp.where(live, values, 0.0).astype(jnp.bfloat16)
    for h in range(q_heads):
        kv = h * kv_heads // q_heads
        cols = slice(kv * HD, (kv + 1) * HD)
        for r in range(n_mp):
            span, seen = slice(r * local_len, (r + 1) * local_len), (r + 1) * local_len
            query = rotated(acc[span, h * HD : (h + 1) * HD], span) * 144.0 ** (-0.5)
            score = lax.dot_general(
                query.astype(jnp.bfloat16),
                key_out[:seen, cols],
                (((1,), (1,)), ((), ())),
                preferred_element_type=jnp.float32,
            )
            row = lax.broadcasted_iota(jnp.int32, score.shape, 0) + r * local_len
            col = lax.broadcasted_iota(jnp.int32, score.shape, 1)
            expo = jnp.exp(50.0 * jnp.tanh(score * (1.0 / 50.0)))
            expo = jnp.where((col <= row) & (col < length), expo, 0.0)
            weights = (expo / jnp.sum(expo, axis=-1, keepdims=True)).astype(jnp.bfloat16)
            att[span, h * HD : (h + 1) * HD] = jnp.dot(
                weights, val_out[:seen, cols], preferred_element_type=jnp.float32
            ).astype(jnp.bfloat16)

    def hand(block, step):
        target = lax.rem(mp + step, n_mp)
        return pltpu.make_async_remote_copy(
            src_ref=psend.at[block, target],
            dst_ref=precv.at[block, n_mp - 1 - step],
            send_sem=psend_sem.at[block, n_mp - 1 - step],
            recv_sem=precv_sem.at[block, n_mp - 1 - step],
            device_id=(me, target),
            device_id_type=MESH,
        )

    def output(block):
        for m in range(n_mp):
            span = slice(m * local_len, (m + 1) * local_len)
            psend[block, m] = jnp.dot(
                att[span, :], obuf[block], preferred_element_type=jnp.float32
            ).astype(jnp.bfloat16)
        for step in range(1, n_mp):
            hand(block, step).start()

    def step_out(k, carry):
        @pl.when((k > 0) & (k < nz))
        def _():
            relay(1, k)

        def each(i, inner):
            other, side = i // 2, i % 2
            distance = k - other
            oz = z + distance * (2 * side - 1)
            origin = oz * 2 + lax.rem(x + other, 2)

            @pl.when(
                (distance >= 0) & (distance < nz) & (oz >= 0) & (oz < nz)
                & ((side == 0) | (distance > 0))
            )
            def _():
                @pl.when(other == 1)
                def _():
                    wait_across(1, origin)

                output(origin)

            return inner

        return lax.fori_loop(0, 4, each, carry)

    lax.fori_loop(0, nz + 1, step_out, 0)

    def summed(block):
        value = psend[block, mp].astype(jnp.float32)
        for slot in range(n_mp - 1):
            value = value + precv[block, slot].astype(jnp.float32)
        return value

    def squares(block, total):
        for step in range(1, n_mp):
            hand(block, step).wait_recv()
        value = summed(block)
        return total + jnp.sum(value * value, axis=-1, keepdims=True)

    total = lax.fori_loop(0, n_dp, squares, jnp.zeros((local_len, 1), jnp.float32))
    scale = lax.rsqrt(total / width + 1e-06)
    own = lax.broadcasted_iota(jnp.int32, (local_len, fcols), 0) + mp * local_len < length
    for block in range(n_dp):
        span = slice(block * fcols, (block + 1) * fcols)
        post = summed(block) * scale * pgain[:, span]
        mixed[:, span] = jnp.where(own, hid[:, span].astype(jnp.float32) + post, 0.0).astype(
            jnp.bfloat16
        )

    drain(0)
    drain(1)
    for step in range(1, n_mp):
        share(step).wait_send()

    def drain_hand(block, carry):
        for step in range(1, n_mp):
            hand(block, step).wait_send()
        return carry

    lax.fori_loop(0, n_dp, drain_hand, 0)


def local(n_dp, n_mp, hidden, lengths, norm_gain, w_query, w_key, w_value, w_out, post_gain):
    _, local_len, width = hidden.shape
    maxlen = local_len * n_mp
    rows, qw = w_query.shape
    kw = w_key.shape[1]
    orows, fcols = w_out.shape
    cuts = (cut(rows), cut(orows))
    cosine, sine = tables(maxlen)
    vmem = pl.BlockSpec(memory_space=pltpu.VMEM)
    anywhere = pl.BlockSpec(memory_space=pl.ANY)
    bf16, f32 = jnp.bfloat16, jnp.float32
    dma = pltpu.SemaphoreType.DMA
    mixed, keys, values = pl.pallas_call(
        functools.partial(kernel, n_dp, n_mp, cuts),
        out_shape=(
            jax.ShapeDtypeStruct((local_len, width), bf16),
            jax.ShapeDtypeStruct((maxlen, kw), bf16),
            jax.ShapeDtypeStruct((maxlen, kw), bf16),
        ),
        in_specs=[pl.BlockSpec(memory_space=pltpu.SMEM), vmem, vmem]
        + [anywhere] * 4
        + [vmem, vmem, vmem],
        out_specs=(vmem, vmem, vmem),
        scratch_shapes=[
            pltpu.VMEM((n_dp, rows, qw + 2 * kw), bf16),
            pltpu.VMEM((n_dp, orows, fcols), bf16),
            pltpu.VMEM((n_mp, n_dp, local_len, fcols), bf16),
            pltpu.VMEM((maxlen, qw + 2 * kw), f32),
            pltpu.VMEM((maxlen, qw), bf16),
            pltpu.VMEM((n_dp, n_mp, local_len, fcols), bf16),
            pltpu.VMEM((n_dp, n_mp - 1, local_len, fcols), bf16),
            dma((4,)),
            dma((2, 3, 3, n_dp)),
            dma((2, 3, n_dp)),
            dma((n_mp,)),
            dma((n_mp,)),
            dma((n_dp, n_mp - 1)),
            dma((n_dp, n_mp - 1)),
        ],
        compiler_params=pltpu.CompilerParams(
            collective_id=0, has_side_effects=True, vmem_limit_bytes=60 * 1024 * 1024
        ),
    )(
        lengths,
        hidden[0],
        norm_gain.reshape(1, width),
        w_query,
        w_key,
        w_value,
        w_out,
        post_gain.reshape(1, width),
        jnp.asarray(cosine),
        jnp.asarray(sine),
    )
    return mixed[None], keys[None], values[None]


def solution(mesh):
    return jax.shard_map(
        functools.partial(local, mesh.shape["dp"], mesh.shape["mp"]),
        mesh=mesh,
        in_specs=(
            P("dp", "mp", None),
            P("dp"),
            P(),
            P("dp", "mp"),
            P("dp", "mp"),
            P("dp", "mp"),
            P("mp", "dp"),
            P(),
        ),
        out_specs=(P("dp", "mp", None), P("dp", None, "mp"), P("dp", None, "mp")),
        check_vma=False,
    )
```

time: 382 us -> 182 us (0.48)
  waiting for transfers between devices: 316 us -> 0 us
  Pallas kernels: 0 us -> 170 us
  matrix products: 23.5 us -> 0 us
  between operations: 14.9 us -> 1.3 us
  other arithmetic: 11.6 us -> 0 us
  local copies, waits for them, and re-layouts: 14.8 us -> 8.66 us
    all_gather x5 -> x0, waiting for transfers between devices: 268 us -> none  [the longest x1 75.2 us: local(): lax.all_gather(w_query, 'dp', axis=0, tiled=True)]
    pallas_call x0 -> x1, Pallas kernels: none -> 170 us  [local(): pl.pallas_call(functools.partial(kernel, n_dp, n_mp, cuts), out_shape=(ja...]
    reduce_scatter x1 -> x0, waiting for transfers between devices: 45.2 us -> none  [local(): lax.psum_scatter(partial_value.reshape(rollouts, maxlen, width).astype(jn...]
    dot_general x5 -> x0, matrix products: 21.6 us -> none  [the longest x3 12.4 us: local(): jnp.dot(flat, piece, preferred_element_type=jnp.float32)]
    dot_general x3 -> x0, local copies, waits for them, and re-layouts: 13.9 us -> none  [local(): jnp.dot(flat, piece, preferred_element_type=jnp.float32)]
    unnamed x8, local copies, waits for them, and re-layouts: 0.02 us -> 5.97 us
    convert_element_type x4 -> x0, other arithmetic: 5.85 us -> none  [the longest x1 2.87 us: local(): mixed = jnp.where(live_local, rows_f + post, 0.0).astype(jnp.bfloat16)]
  transfers between devices with their start and end apart: 6 -> 0, of which waited for: 6 -> 0; matrix products, arithmetic and copies ran while one was open for 10% -> 0% of each run, Pallas kernels for 0% -> 0%
where the time goes in v1:
time: 182 us; the launch traced here: 180 us
  Pallas kernels  170 us (93%)
  local copies, waits for them, and re-layouts  8.66 us (5%)
    pallas_call x1, Pallas kernels, local(): pl.pallas_call(functools.partial(kernel, n_dp, n_mp, cuts), out_shape=(ja...  170 us
    unnamed x8, local copies, waits for them, and re-layouts  5.97 us

profile of v1, /device:TPU:0, one launch (start us, length us, event | category | flops | bytes accessed | tf_op | source)
XLA Modules:
  0.0 180.3 jit_solution(13780751671525628056)
XLA Ops:
  1.3 1.3 reshape.12.ngain
  2.6 1.3 reshape.13.pgain
  4.0 2.1 %copy.13.wo = bf16[512,576]{1,0:T(8,128)(2,1)} copy(bf16[512,576]{0,1:T(8,128)(2,1)} %param.16) | data formatting | bytes 1179648 | tf_op args[6]
  6.1 170.4 %shard_map.121 = (bf16[128,4608]{1,0:T(8,128)(2,1)}, bf16[512,256]{1,0:T(8,128)(2,1)}, bf16[512,256]{1,0:T(8,128)(2,1)}) custom-call(s32[1]{0:T(128)S(6)} %copy.17.len_ref, bf16[128,4608]{1,0:T(8,128)(2,1)} %bitcast.4, f32[1,4608]{1,0:T(1,128)} %reshape.12.ngain, bf16[576,512]{1,0:T(8,128)(2,1)} %wq.1, bf16[576,256]{1,0:T(8,128)(2,1)} %wk.1, ...), custom_call_target="tpu_custom_call" | custom-call | tf_op jit(solution)/shard_map/pallas_call | solution.py:397
  176.5 0.0 copy-start.1
  176.5 0.0 copy-start
  176.5 2.4 %copy.18 = bf16[1,128,4608]{2,1,0:T(8,128)(2,1)} copy(bf16[1,128,4608]{2,1,0:T(8,128)(2,1)} %bitcast.5) | data formatting | bytes 2359296
  178.9 0.0 copy-done.1
  178.9 0.7 copy.19
  179.6 0.0 copy-done
  179.6 0.7 copy.20
Async XLA Ops:
  176.5 2.4 %copy-start.1 = (bf16[512,256]{1,0:T(8,128)(2,1)S(1)}, bf16[512,256]{1,0:T(8,128)(2,1)}, u32[]{:S(2)}) copy-start(bf16[512,256]{1,0:T(8,128)(2,1)} %get-tuple-element.7) | copy-start | bytes 786436
  176.5 3.1 %copy-start = (bf16[512,256]{1,0:T(8,128)(2,1)S(1)}, bf16[512,256]{1,0:T(8,128)(2,1)}, u32[]{:S(2)}) copy-start(bf16[512,256]{1,0:T(8,128)(2,1)} %get-tuple-element.8) | copy-start | bytes 786436

commit v2 on v1

--- a/solution.py
+++ b/solution.py
@@ -263,7 +263,6 @@
         return carry
 
     lax.fori_loop(0, 4 * nz, project, 0)
-    send_partner(1)
 
     length = len_ref[0]
     live = lax.broadcasted_iota(jnp.int32, (maxlen, HD), 0) < length
@@ -279,6 +278,9 @@
         values = acc[:, qw + kw + h * HD : qw + kw + (h + 1) * HD]
         val_out[:, cols] = jnp.where(live, values, 0.0).astype(jnp.bfloat16)
     for h in range(q_heads):
+        if h == q_heads // 2:
+            send_partner(1)
+            relay(1, 1)
         kv = h * kv_heads // q_heads
         cols = slice(kv * HD, (kv + 1) * HD)
         for r in range(n_mp):
@@ -320,7 +322,7 @@
             hand(block, step).start()
 
     def step_out(k, carry):
-        @pl.when((k > 0) & (k < nz))
+        @pl.when((k > 1) & (k < nz))
         def _():
             relay(1, k)
 

time: 182 us -> 187 us (1.027)
  Pallas kernels: 170 us -> 175 us
    pallas_call x1, Pallas kernels: 170 us -> 175 us  [local(): pl.pallas_call(functools.partial(kernel, n_dp, n_mp, cuts), out_shape=(ja...]
where the time goes in v2:
time: 187 us; the launch traced here: 185 us
  Pallas kernels  175 us (94%)
  local copies, waits for them, and re-layouts  8.66 us (5%)
    pallas_call x1, Pallas kernels, local(): pl.pallas_call(functools.partial(kernel, n_dp, n_mp, cuts), out_shape=(ja...  175 us
    unnamed x8, local copies, waits for them, and re-layouts  5.97 us

profile of v2, /device:TPU:0, one launch (start us, length us, event | category | flops | bytes accessed | tf_op | source)
XLA Modules:
  0.0 185.1 jit_solution(2729121124572042702)
XLA Ops:
  1.3 1.3 reshape.12.ngain
  2.6 1.3 reshape.13.pgain
  4.0 2.1 %copy.13.wo = bf16[512,576]{1,0:T(8,128)(2,1)} copy(bf16[512,576]{0,1:T(8,128)(2,1)} %param.16) | data formatting | bytes 1179648 | tf_op args[6]
  6.1 175.1 %shard_map.121 = (bf16[128,4608]{1,0:T(8,128)(2,1)}, bf16[512,256]{1,0:T(8,128)(2,1)}, bf16[512,256]{1,0:T(8,128)(2,1)}) custom-call(s32[1]{0:T(128)S(6)} %copy.17.len_ref, bf16[128,4608]{1,0:T(8,128)(2,1)} %bitcast.4, f32[1,4608]{1,0:T(1,128)} %reshape.12.ngain, bf16[576,512]{1,0:T(8,128)(2,1)} %wq.1, bf16[576,256]{1,0:T(8,128)(2,1)} %wk.1, ...), custom_call_target="tpu_custom_call" | custom-call | tf_op jit(solution)/shard_map/pallas_call | solution.py:399
  181.2 0.0 copy-start.1
  181.2 0.0 copy-start
  181.2 2.4 %copy.18 = bf16[1,128,4608]{2,1,0:T(8,128)(2,1)} copy(bf16[1,128,4608]{2,1,0:T(8,128)(2,1)} %bitcast.5) | data formatting | bytes 2359296
  183.6 0.0 copy-done.1
  183.6 0.7 copy.19
  184.3 0.0 copy-done
  184.3 0.7 copy.20
Async XLA Ops:
  181.2 2.4 %copy-start.1 = (bf16[512,256]{1,0:T(8,128)(2,1)S(1)}, bf16[512,256]{1,0:T(8,128)(2,1)}, u32[]{:S(2)}) copy-start(bf16[512,256]{1,0:T(8,128)(2,1)} %get-tuple-element.7) | copy-start | bytes 786436
  181.2 3.1 %copy-start = (bf16[512,256]{1,0:T(8,128)(2,1)S(1)}, bf16[512,256]{1,0:T(8,128)(2,1)}, u32[]{:S(2)}) copy-start(bf16[512,256]{1,0:T(8,128)(2,1)} %get-tuple-element.8) | copy-start | bytes 786436

commit v3 on v1

--- a/solution.py
+++ b/solution.py
@@ -37,8 +37,8 @@
     n_dp, n_mp, cuts,
     len_ref, hid, ngain, wq, wk, wv, wo, pgain, cos_ref, sin_ref,
     mixed, key_out, val_out,
-    wbuf, obuf, nbuf, acc, att, psend, precv,
-    load_sem, send_sem, recv_sem, nsend_sem, nrecv_sem, psend_sem, precv_sem,
+    wbuf, obuf, nbuf, acc, att, psend, precv, inbox,
+    load_sem, send_sem, recv_sem, nsend_sem, nrecv_sem, psend_sem, precv_sem, fsend_sem, inbox_sem,
 ):
     nz = n_dp // 2
     me, mp = lax.axis_index("dp"), lax.axis_index("mp")
@@ -299,16 +299,40 @@
                 weights, val_out[:seen, cols], preferred_element_type=jnp.float32
             ).astype(jnp.bfloat16)
 
+    pairs = n_mp // 2
+    mate = mp + 1 - 2 * lax.rem(mp, 2)
+
     def hand(block, step):
-        target = lax.rem(mp + step, n_mp)
+        part = lax.rem(mate + 2 * step, n_mp)
+        return pltpu.make_async_remote_copy(
+            src_ref=psend.at[block, part],
+            dst_ref=precv.at[block, 0] if step == 0 else inbox.at[block, step - 1],
+            send_sem=psend_sem.at[block, step],
+            recv_sem=precv_sem.at[block, 0] if step == 0 else inbox_sem.at[block, step - 1],
+            device_id=(me, mate),
+            device_id_type=MESH,
+        )
+
+    def far(block, step):
+        target = lax.rem(mp + 2 * step, n_mp)
         return pltpu.make_async_remote_copy(
             src_ref=psend.at[block, target],
-            dst_ref=precv.at[block, n_mp - 1 - step],
-            send_sem=psend_sem.at[block, n_mp - 1 - step],
-            recv_sem=precv_sem.at[block, n_mp - 1 - step],
+            dst_ref=precv.at[block, pairs - step],
+            send_sem=fsend_sem.at[block, step - 1],
+            recv_sem=precv_sem.at[block, pairs - step],
             device_id=(me, target),
             device_id_type=MESH,
         )
+
+    def forward(block):
+        for step in range(1, pairs):
+            hand(block, step).wait_recv()
+            target = lax.rem(mp + 2 * step, n_mp)
+            both = psend[block, target].astype(jnp.float32) + inbox[block, step - 1].astype(
+                jnp.float32
+            )
+            psend[block, target] = both.astype(jnp.bfloat16)
+            far(block, step).start()
 
     def output(block):
         for m in range(n_mp):
@@ -316,7 +340,7 @@
             psend[block, m] = jnp.dot(
                 att[span, :], obuf[block], preferred_element_type=jnp.float32
             ).astype(jnp.bfloat16)
-        for step in range(1, n_mp):
+        for step in list(range(1, pairs)) + [0]:
             hand(block, step).start()
 
     def step_out(k, carry):
@@ -340,6 +364,7 @@
                     wait_across(1, origin)
 
                 output(origin)
+                forward(origin)
 
             return inner
 
@@ -349,13 +374,14 @@
 
     def summed(block):
         value = psend[block, mp].astype(jnp.float32)
-        for slot in range(n_mp - 1):
+        for slot in range(pairs):
             value = value + precv[block, slot].astype(jnp.float32)
         return value
 
     def squares(block, total):
-        for step in range(1, n_mp):
-            hand(block, step).wait_recv()
+        hand(block, 0).wait_recv()
+        for step in range(1, pairs):
+            far(block, step).wait_recv()
         value = summed(block)
         return total + jnp.sum(value * value, axis=-1, keepdims=True)
 
@@ -375,8 +401,10 @@
         share(step).wait_send()
 
     def drain_hand(block, carry):
-        for step in range(1, n_mp):
+        for step in range(pairs):
             hand(block, step).wait_send()
+        for step in range(1, pairs):
+            far(block, step).wait_send()
         return carry
 
     lax.fori_loop(0, n_dp, drain_hand, 0)
@@ -412,14 +440,17 @@
             pltpu.VMEM((maxlen, qw + 2 * kw), f32),
             pltpu.VMEM((maxlen, qw), bf16),
             pltpu.VMEM((n_dp, n_mp, local_len, fcols), bf16),
-            pltpu.VMEM((n_dp, n_mp - 1, local_len, fcols), bf16),
+            pltpu.VMEM((n_dp, n_mp // 2, local_len, fcols), bf16),
+            pltpu.VMEM((n_dp, n_mp // 2 - 1, local_len, fcols), bf16),
             dma((4,)),
             dma((2, 3, 3, n_dp)),
             dma((2, 3, n_dp)),
             dma((n_mp,)),
             dma((n_mp,)),
-            dma((n_dp, n_mp - 1)),
-            dma((n_dp, n_mp - 1)),
+            dma((n_dp, n_mp // 2)),
+            dma((n_dp, n_mp // 2)),
+            dma((n_dp, n_mp // 2 - 1)),
+            dma((n_dp, n_mp // 2 - 1)),
         ],
         compiler_params=pltpu.CompilerParams(
             collective_id=0, has_side_effects=True, vmem_limit_bytes=60 * 1024 * 1024

time: 182 us -> 173 us (0.951)
  Pallas kernels: 170 us -> 163 us
    pallas_call x1, Pallas kernels: 170 us -> 163 us  [local(): pl.pallas_call(functools.partial(kernel, n_dp, n_mp, cuts), out_shape=(ja...]
where the time goes in v3:
time: 173 us
  Pallas kernels  163 us (94%)
  local copies, waits for them, and re-layouts  8.66 us (5%)
    pallas_call x1, Pallas kernels, local(): pl.pallas_call(functools.partial(kernel, n_dp, n_mp, cuts), out_shape=(ja...  163 us
    unnamed x8, local copies, waits for them, and re-layouts  5.97 us

profile of v3, /device:TPU:0, one launch (start us, length us, event | category | flops | bytes accessed | tf_op | source)
XLA Modules:
  0.0 172.6 jit_solution(8630637121706815162)
XLA Ops:
  1.3 1.3 reshape.12.ngain
  2.6 1.3 reshape.13.pgain
  4.0 2.1 %copy.13.wo = bf16[512,576]{1,0:T(8,128)(2,1)} copy(bf16[512,576]{0,1:T(8,128)(2,1)} %param.16) | data formatting | bytes 1179648 | tf_op args[6]
  6.1 162.6 %shard_map.121 = (bf16[128,4608]{1,0:T(8,128)(2,1)}, bf16[512,256]{1,0:T(8,128)(2,1)}, bf16[512,256]{1,0:T(8,128)(2,1)}) custom-call(s32[1]{0:T(128)S(6)} %copy.17.len_ref, bf16[128,4608]{1,0:T(8,128)(2,1)} %bitcast.4, f32[1,4608]{1,0:T(1,128)} %reshape.12.ngain, bf16[576,512]{1,0:T(8,128)(2,1)} %wq.1, bf16[576,256]{1,0:T(8,128)(2,1)} %wk.1, ...), custom_call_target="tpu_custom_call" | custom-call | tf_op jit(solution)/shard_map/pallas_call | solution.py:425
  168.7 0.0 copy-start.1
  168.7 0.0 copy-start
  168.7 2.4 %copy.18 = bf16[1,128,4608]{2,1,0:T(8,128)(2,1)} copy(bf16[1,128,4608]{2,1,0:T(8,128)(2,1)} %bitcast.5) | data formatting | bytes 2359296
  171.2 0.0 copy-done.1
  171.2 0.7 copy.19
  171.9 0.0 copy-done
  171.9 0.7 copy.20
Async XLA Ops:
  168.7 2.4 %copy-start.1 = (bf16[512,256]{1,0:T(8,128)(2,1)S(1)}, bf16[512,256]{1,0:T(8,128)(2,1)}, u32[]{:S(2)}) copy-start(bf16[512,256]{1,0:T(8,128)(2,1)} %get-tuple-element.7) | copy-start | bytes 786436
  168.7 3.1 %copy-start = (bf16[512,256]{1,0:T(8,128)(2,1)S(1)}, bf16[512,256]{1,0:T(8,128)(2,1)}, u32[]{:S(2)}) copy-start(bf16[512,256]{1,0:T(8,128)(2,1)} %get-tuple-element.8) | copy-start | bytes 786436
